TPU v7x, 32 devices: a whole 2x2x4 slice. The times are simulated.
32 devices in a mesh: rows: 8 (over y, x, core), cols: 4 (over z).
Axes of the slice: x: 2, y: 2, z: 4, core: 2. Of those that a mesh axis runs over, the one named last changes fastest.
Arguments:
- token_ids: int32 [16, 2048], P('rows', 'cols'), may hold values from 0 to 131071, as said below
- lengths: int32 [16], P('rows'), may hold values from 1 to 2048
- table: bfloat16 [131072, 512], P('rows', 'cols'), may hold values from -6 to 6
- attn_gain: float32 [512], replicated, may hold values from 0.1 to 1.9
- w_qkv: bfloat16 [512, 1536], replicated, may hold values from -2 to 2
- w_out: bfloat16 [512, 512], replicated, may hold values from -0.25 to 0.25
- mlp_gain: float32 [512], replicated, may hold values from 0.1 to 1.9
- w_in: bfloat16 [512, 4096], replicated, may hold values from -0.25 to 0.25
- w_down: bfloat16 [2048, 512], replicated, may hold values from -0.125 to 0.125
Outputs:
- layer_out: bfloat16 [16, 2048, 512], P('rows', 'cols')
Inputs may be any that keep to these rules, and one draw needn't show every extreme that they name: `token_ids`: ids lie in 0 to 131071. In each aligned block of 2 histories (4096 positions) at most 1365 ids fall in any one block of 16384 consecutive table rows, and in every such block of histories some block of table rows receives exactly 1365.
All inputs are finite; a program needn't handle non-finite values.
Results may differ from a plain program's by a relative error of at most 0.012.
Values may be sent and summed in bfloat16 or wider, within the bound.
A program may use at most 192 MiB of HBM per device.

v0:
```python
import jax
import jax.numpy as jnp
from jax import lax
from jax.sharding import PartitionSpec as P

D = 512
HEADS = 8
FF = 2048


def rms_norm(values_f32, gain):
    mean_sq = jnp.mean(values_f32 * values_f32, axis=-1, keepdims=True)
    return values_f32 * lax.rsqrt(mean_sq + 1e-06) * gain


def local(token_ids, lengths, table, attn_gain, w_qkv, w_out, mlp_gain, w_in, w_down):
    batch_dev, quarter = token_ids.shape
    col_count = lax.axis_size("cols")
    row_count = lax.axis_size("rows")
    full_len = quarter * col_count
    block_rows, col_width = table.shape
    zero_bf = jnp.zeros((), jnp.bfloat16)
    own_ids = lax.all_gather(token_ids, "cols", axis=1, tiled=True)
    flat_ids = own_ids.reshape(-1)
    token_count = flat_ids.shape[0]
    capacity = 8 * token_count // (3 * row_count)
    owner_block = flat_ids // block_rows
    onehot = (owner_block[:, None] == jnp.arange(row_count, dtype=jnp.int32)[None, :]).astype(
        jnp.int32
    )
    slot_rank = jnp.sum((jnp.cumsum(onehot, axis=0) - 1) * onehot, axis=1)
    slot_index = owner_block * capacity + slot_rank
    requests = jnp.full((row_count * capacity,), -1, jnp.int32)
    requests = (
        requests.at[slot_index]
        .set(flat_ids - owner_block * block_rows)
        .reshape(row_count, capacity)
    )
    asked = lax.all_to_all(requests, "rows", split_axis=0, concat_axis=0, tiled=True)
    looked = jnp.take(table, jnp.maximum(asked, 0), axis=0)
    looked = jnp.where((asked >= 0)[..., None], looked, zero_bf)
    returned = lax.all_to_all(looked, "rows", split_axis=0, concat_axis=0, tiled=True)
    embedded = returned.reshape(row_count * capacity, col_width)[slot_index]
    embedded = embedded.reshape(batch_dev, full_len, col_width)
    sequence = lax.all_to_all(embedded, "cols", split_axis=1, concat_axis=2, tiled=True)
    residual = sequence.astype(jnp.float32)
    normed = rms_norm(residual, attn_gain).astype(jnp.bfloat16)
    projected = jnp.einsum("bqe,ef->bqf", normed, w_qkv, preferred_element_type=jnp.float32).astype(
        jnp.bfloat16
    )
    head_dim = D // HEADS
    queries = projected[..., :D].reshape(batch_dev, quarter, HEADS, head_dim)
    keys = projected[..., D : 2 * D]
    values = projected[..., 2 * D :]
    query_pos = lax.axis_index("cols") * quarter + jnp.arange(quarter, dtype=jnp.int32)
    running_max = jnp.full((batch_dev, HEADS, quarter), -1e30, jnp.float32)
    key_piece = lax.all_gather(keys, "cols", axis=1, tiled=True)
    value_piece = lax.all_gather(values, "cols", axis=1, tiled=True)
    piece_len = key_piece.shape[1]
    key_heads = key_piece.reshape(batch_dev, piece_len, HEADS, head_dim)
    value_heads = value_piece.reshape(batch_dev, piece_len, HEADS, head_dim)
    scores = (
        jnp.einsum("bqhd,bkhd->bhqk", queries, key_heads, preferred_element_type=jnp.float32)
        * 0.125
    )
    key_pos = jnp.arange(piece_len, dtype=jnp.int32)
    causal = key_pos[None, :] <= query_pos[:, None]
    inside = key_pos[None, :] < lengths[:, None]
    valid = causal[None, None, :, :] & inside[:, None, None, :]
    scores = jnp.where(valid, scores, -1e30)
    new_max = jnp.maximum(running_max, jnp.max(scores, axis=-1))
    probs = jnp.where(valid, jnp.exp(scores - new_max[..., None]), 0.0)
    running_sum = jnp.sum(probs, axis=-1)
    weighted = jnp.einsum(
        "bhqk,bkhd->bhqd",
        probs.astype(jnp.bfloat16),
        value_heads,
        preferred_element_type=jnp.float32,
    )
    final_max, final_sum, weighted = (new_max, running_sum, weighted)
    summed = weighted / final_sum[..., None]
    attended = (
        jnp.transpose(summed, (0, 2, 1, 3)).reshape(batch_dev, quarter, D).astype(jnp.bfloat16)
    )
    hidden = (
        residual + jnp.einsum("bqe,ef->bqf", attended, w_out, preferred_element_type=jnp.float32)
    ).astype(jnp.bfloat16)
    hidden_f32 = hidden.astype(jnp.float32)
    normed_two = rms_norm(hidden_f32, mlp_gain).astype(jnp.bfloat16)
    gate_up = jnp.einsum("bqe,ef->bqf", normed_two, w_in, preferred_element_type=jnp.float32)
    act = (jax.nn.silu(gate_up[..., :FF]) * gate_up[..., FF:]).astype(jnp.bfloat16)
    return (
        hidden_f32 + jnp.einsum("bqf,fe->bqe", act, w_down, preferred_element_type=jnp.float32)
    ).astype(jnp.bfloat16)


def solution(mesh):
    in_specs = (P("rows", "cols"), P("rows"), P("rows", "cols"), P(), P(), P(), P(), P(), P())
    out_specs = P("rows", "cols", None)
    return jax.shard_map(local, mesh=mesh, in_specs=in_specs, out_specs=out_specs, check_vma=False)
```

profile of v0, /device:TPU:0, one launch (start us, length us, event | category | flops | bytes accessed | tf_op | source)
XLA Modules:
  0.0 414.5 jit_solution(13161058633130101524)
XLA Ops:
  6.5 15.2 %all_gather.9 = s32[2,2048]{1,0:T(2,128)S(1)} all-gather(s32[2,512]{1,0:T(2,128)} %param.9), channel_id=1, replica_groups=mesh['rows'=8,'cols'=4] {'cols'}, dimensions={1}, use_global_device_ids=true | all-gather | bytes 20480 | tf_op jit(solution)/shard_map/all_gather | solution.py:23
  21.8 2.3 reduce-window.6
  25.0 15.5 %scatter_custom_fusion = s32[10920]{0:T(1024)S(1)} fusion(s32[4096]{0:T(1024)S(1)} %bitcast.81, s32[4096]{0:T(1024)S(1)} %get-tuple-element.10, s32[]{:T(128)} %constant.27.clone.1), kind=kCustom, calls=%fused_computation.65 | custom fusion | bytes 43684 | tf_op jit(solution)/shard_map/scatter | solution.py:36
  40.6 8.4 %all_to_all.23 = s32[8,1,1365]{2,1,0:T(1,128)S(1)} all-to-all(s32[8,1,1365]{2,1,0:T(1,128)S(1)} %all_to_all.16), channel_id=1, replica_groups=mesh['rows'=8,'cols'=4] {'rows'}, dimensions={0} | all-to-all | bytes 87360 | tf_op jit(solution)/shard_map/all_to_all | solution.py:39
  49.2 23.7 %gather_fusion = bf16[10920,128]{1,0:T(8,128)(2,1)} fusion(bf16[16384,128]{1,0:T(8,128)(2,1)} %param.11, s32[11264]{0:T(1024)S(1)} %pad_clamp_fusion), kind=kCustom, calls=%fused_computation | custom fusion | bytes 5634720 | tf_op jit(solution)/shard_map/jit(_take)/gather | solution.py:40
  72.9 4.2 %reshape.264 = bf16[8,1365,128]{2,1,0:T(8,128)(2,1)} reshape(bf16[10920,128]{1,0:T(8,128)(2,1)} %gather_fusion) | data formatting | bytes 5591040 | tf_op jit(solution)/shard_map/jit(_take)/gather | solution.py:40
  77.1 10.2 %select_select_fusion = bf16[8,1365,128]{2,1,0:T(8,128)(2,1)} fusion(bf16[8,1365,128]{2,1,0:T(8,128)(2,1)} %reshape.264, pred[8,1365]{1,0:T(8,128)(4,1)S(1)} %get-tuple-element.9, pred[8,1365]{1,0:T(8,128)(4,1)S(1)} %get-tuple-element.8), kind=kLoop, calls=%fused_computation.21 | loop fusion | flops 2795520 | bytes 5612880 | tf_op jit(solution)/shard_map/jit(_where)/select_n | solution.py:41
  87.3 4.4 %all-to-all-start.1 = ((bf16[8,1365,128]{2,1,0:T(8,128)(2,1)}), bf16[8,1365,128]{2,1,0:T(8,128)(2,1)}, u32[]{:S(2)}, u32[]{:S(2)}) async-start(bf16[8,1365,128]{2,1,0:T(8,128)(2,1)} %select_select_fusion), calls=%async_computation.1 | async-start | bytes 5603328 | tf_op jit(solution)/shard_map/all_to_all | solution.py:42
  91.8 34.1 %all-to-all-done.1 = bf16[8,1365,128]{2,1,0:T(8,128)(2,1)} async-done(((bf16[8,1365,128]{2,1,0:T(8,128)(2,1)}), bf16[8,1365,128]{2,1,0:T(8,128)(2,1)}, u32[]{:S(2)}, u32[]{:S(2)}) %all-to-all-start.1) | async-done | bytes 2795552 | tf_op jit(solution)/shard_map/all_to_all | solution.py:42
  125.9 4.2 %reshape.256 = bf16[10920,128]{1,0:T(8,128)(2,1)} reshape(bf16[8,1365,128]{2,1,0:T(8,128)(2,1)} %all-to-all-done.1) | data formatting | bytes 5591040 | tf_op jit(solution)/shard_map/reshape | solution.py:43
  130.1 13.2 %gather_fusion.1 = bf16[4096,128]{1,0:T(8,128)(2,1)S(1)} fusion(bf16[10920,128]{1,0:T(8,128)(2,1)} %reshape.256, s32[4096]{0:T(1024)S(1)} %broadcast_clamp_fusion), kind=kCustom, calls=%fused_computation.1 | custom fusion | bytes 2113536 | tf_op jit(solution)/shard_map/gather | solution.py:43
  143.3 8.7 %copy.57 = bf16[2,2048,128]{2,0,1:T(2,128)(2,1)S(1)} copy(bf16[2,2048,128]{2,1,0:T(8,128)(2,1)S(1)} %bitcast.75) | data formatting | bytes 2097152 | tf_op jit(solution)/shard_map/reshape | solution.py:44
  152.0 27.2 %all_to_all.24 = bf16[2,2048,128]{2,0,1:T(2,128)(2,1)S(1)} all-to-all(bf16[2,2048,128]{2,0,1:T(2,128)(2,1)S(1)} %copy.57), channel_id=1, replica_groups=mesh['rows'=8,'cols'=4] {'cols'}, dimensions={1} | all-to-all | bytes 2097152 | tf_op jit(solution)/shard_map/all_to_all | solution.py:45
  179.2 1.5 copy_convert_fusion
  180.7 2.9 copy.59
  184.3 1.8 fusion.18
  186.2 3.2 convolution_convert_fusion
  189.4 1.7 fusion.44
  191.3 0.7 iota_compare_fusion
  191.9 2.6 broadcast_and_fusion
  194.6 1.3 copy.61
  195.9 76.4 %all-gather.3.cloned.1.call-done = bf16[2,2048,512]{2,1,0:T(8,128)(2,1)} async-done(((bf16[2,512,512]{2,1,0:T(8,128)(2,1)}), bf16[2,2048,512]{2,1,0:T(8,128)(2,1)}) %all-gather.3.cloned.1.call-update) | async-done | bytes 4194320 | tf_op jit(solution)/shard_map/all_gather | solution.py:57
  272.4 6.3 %copy.62 = bf16[2,2048,512]{1,2,0:T(8,128)(2,1)} copy(bf16[2,2048,512]{2,1,0:T(8,128)(2,1)} %all-gather.3.cloned.1.call-done) | data formatting | bytes 8388608 | tf_op jit(solution)/shard_map/all_gather | solution.py:57
  278.6 27.7 %fusion = (f32[2,8,512]{2,1,0:T(8,128)S(1)}, f32[2,8,512,2048]{3,2,1,0:T(8,128)}) fusion(pred[2,512,2048]{2,1,0:T(8,128)(4,1)} %broadcast_and_fusion, bf16[2,512,8,64]{1,3,2,0:T(8,128)(2,1)} %bitcast.74, bf16[2,2048,8,64]{1,3,2,0:T(8,128)(2,1)} %bitcast.72), kind=kOutput, calls=%fused_computation.5 | convolution fusion | flops 2197807104 | bytes 74481664 | tf_op jit(solution)/shard_map/bqhd,bkhd->bhqk/dot_general | solution.py:63
  306.3 22.4 %fusion.1 = f32[2,8,512]{2,1,0:T(8,128)S(1)} fusion(f32[2,8,512,2048]{3,2,1,0:T(8,128)} %get-tuple-element.13, f32[2,8,512]{2,1,0:T(8,128)S(1)} %broadcast_maximum_fusion, pred[2,512,2048]{2,1,0:T(8,128)(4,1)S(1)} %copy-done.1), kind=kLoop, calls=%fused_computation.6 | loop fusion | flops 83877888 | bytes 69271552 | tf_op jit(solution)/shard_map/reduce_sum | solution.py:73
  328.7 24.5 %all-gather.5.cloned.1.call-done = bf16[2,2048,512]{2,1,0:T(8,128)(2,1)} async-done(((bf16[2,512,512]{2,1,0:T(8,128)(2,1)}), bf16[2,2048,512]{2,1,0:T(8,128)(2,1)}) %all-gather.5.cloned.1.call-update) | async-done | bytes 4194320 | tf_op jit(solution)/shard_map/all_gather | solution.py:58
  353.2 6.3 %copy.63 = bf16[2,2048,512]{1,2,0:T(8,128)(2,1)} copy(bf16[2,2048,512]{2,1,0:T(8,128)(2,1)} %all-gather.5.cloned.1.call-done) | data formatting | bytes 8388608 | tf_op jit(solution)/shard_map/all_gather | solution.py:58
  359.5 27.0 %fusion.16 = bf16[2,512,8,64]{1,3,2,0:T(8,128)(2,1)S(1)} fusion(bf16[2,2048,8,64]{1,3,2,0:T(8,128)(2,1)} %bitcast.76, f32[2,8,512,2048]{3,2,1,0:T(8,128)} %get-tuple-element.13, f32[2,8,512]{2,1,0:T(8,128)S(1)} %broadcast_maximum_fusion, pred[2,512,2048]{2,1,0:T(8,128)(4,1)} %broadcast_and_fusion, f32[2,512,8]{1,2,0:T(8,128)S(1)} %bitcast.85), kind=kOutput, calls=%fused_computation.28 | convolution fusion | flops 2232418304 | bytes 74514432 | tf_op jit(solution)/shard_map/bhqk,bkhd->bhqd/dot_general | solution.py:74
  386.5 2.7 fusion.11
  389.4 8.3 %fusion.7 = f32[2,512,4096]{2,1,0:T(8,128)} fusion(bf16[512,4096]{1,0:T(8,128)(2,1)S(1)} %copy-done.4, bf16[2,512,512]{1,2,0:T(8,128)(2,1)S(1)} %get-tuple-element.15, f32[512]{0:T(512)S(1)} %copy-done.5, f32[2,512]{1,0:T(2,128)S(1)} %add_rsqrt_fusion), kind=kOutput, calls=%fused_computation.12 | convolution fusion | flops 4297064448 | bytes 22026240 | tf_op jit(solution)/shard_map/bqe,ef->bqf/dot_general | solution.py:90
  397.8 8.6 %fusion.14 = bf16[2,512,512]{1,2,0:T(8,128)(2,1)S(1)} fusion(bf16[2,512,512]{1,2,0:T(8,128)(2,1)S(1)} %get-tuple-element.15, bf16[2048,512]{1,0:T(8,128)(2,1)S(1)} %copy-done, f32[2,512,4096]{2,1,0:T(8,128)} %fusion.7), kind=kOutput, calls=%fused_computation.25 | convolution fusion | flops 2161639424 | bytes 20971520 | tf_op jit(solution)/shard_map/bqf,fe->bqe/dot_general | solution.py:93
  406.3 1.3 copy.68
  (41 shorter events, 2.3 us)
Async XLA Ops:
  6.5 391.2 %copy-start = (bf16[2048,512]{1,0:T(8,128)(2,1)S(1)}, bf16[2048,512]{1,0:T(8,128)(2,1)}, u32[]{:S(2)}) copy-start(bf16[2048,512]{1,0:T(8,128)(2,1)} %param.17) | copy-start | bytes 6291460
  87.3 38.6 %all-to-all-start.1 = ((bf16[8,1365,128]{2,1,0:T(8,128)(2,1)}), bf16[8,1365,128]{2,1,0:T(8,128)(2,1)}, u32[]{:S(2)}, u32[]{:S(2)}) async-start(bf16[8,1365,128]{2,1,0:T(8,128)(2,1)} %select_select_fusion), calls=%async_computation.1 | async-start | bytes 5603328 | tf_op jit(solution)/shard_map/all_to_all | solution.py:42
  91.7 180.7 %all-gather.3.cloned.1.call-start = ((), (), s32[]{:S(2)}) async-start(), calls=%async_computation.3 | async-start | bytes 5242880 | tf_op jit(solution)/shard_map/all_gather | solution.py:57
  179.2 5.1 %copy-start.2 = (f32[512]{0:T(512)S(1)}, f32[512]{0:T(512)}, u32[]{:S(2)}) copy-start(f32[512]{0:T(512)} %param.12) | copy-start | bytes 6148
  189.4 1.8 copy-start.3
  191.1 162.1 %all-gather.5.cloned.1.call-start = ((), (), s32[]{:S(2)}) async-start(), calls=%async_computation.4 | async-start | bytes 5242880 | tf_op jit(solution)/shard_map/all_gather | solution.py:58
  278.6 27.7 %copy-start.1 = (pred[2,512,2048]{2,1,0:T(8,128)(4,1)S(1)}, pred[2,512,2048]{2,1,0:T(8,128)(4,1)}, u32[]{:S(2)}) copy-start(pred[2,512,2048]{2,1,0:T(8,128)(4,1)} %broadcast_and_fusion) | copy-start | bytes 6291460
  386.5 3.0 copy-start.4
  386.5 3.0 copy-start.5
Sparse Core Ops, SparseCore 0:
  191.2 81.0 all-gather.2
  273.9 79.2 all-gather.4
where the time goes:
time: 415 us
  waiting for transfers between devices  135 us (33%)
  local copies, waits for them, and re-layouts  90.2 us (22%)
  matrix products  77.4 us (19%)
  blocking collectives  50.8 us (12%)
  other arithmetic  42.8 us (10%)
  between operations  13.7 us (3%)
  starting transfers between devices  4.49 us (1%)
    all_gather x1, waiting for transfers between devices, local(): key_piece = lax.all_gather(keys, 'cols', axis=1, tiled=True)  76.4 us
    all_to_all x1, waiting for transfers between devices, local(): lax.all_to_all(looked, 'rows', split_axis=0, concat_axis=0, tiled=True)  34.1 us
    gather x2, local copies, waits for them, and re-layouts, local(): looked = jnp.take(table, jnp.maximum(asked, 0), axis=0)  27.9 us
    dot_general x1, matrix products, local(): jnp.einsum('bqhd,bkhd->bhqk', queries, key_heads, preferred_element_type=...  27.7 us
    all_to_all x1, blocking collectives, local(): lax.all_to_all(embedded, 'cols', split_axis=1, concat_axis=2, tiled=True)  27.2 us
    dot_general x1, matrix products, local(): jnp.einsum('bhqk,bkhd->bhqd', probs.astype(jnp.bfloat16), value_heads, pr...  27 us
    all_gather x1, waiting for transfers between devices, local(): value_piece = lax.all_gather(values, 'cols', axis=1, tiled=True)  24.5 us
    reduce_sum x1, other arithmetic, local(): running_sum = jnp.sum(probs, axis=-1)  22.4 us
  transfers between devices with their start and end apart: 3, of which 3 were waited for; matrix products, arithmetic and copies ran while one was open for 15% of the time, Pallas kernels for 0%

commit v1 on v0

--- a/solution.py
+++ b/solution.py
@@ -6,6 +6,29 @@
 D = 512
 HEADS = 8
 FF = 2048
+
+
+def cut_along(value, dim, size):
+    lengths = value.shape
+    tiles = value.reshape(*lengths[:dim], size, lengths[dim] // size, *lengths[dim + 1 :])
+    return jnp.moveaxis(tiles, dim, 0)
+
+
+def laid_out(blocks, dim):
+    shape = list(blocks.shape[1:])
+    shape[dim] *= blocks.shape[0]
+    return jnp.moveaxis(blocks, 0, dim).reshape(shape)
+
+
+def exchange_directly(x, axis, split_dim, concat_dim):
+    size, index = (lax.axis_size(axis), lax.axis_index(axis))
+    blocks = cut_along(x, split_dim, size)
+    done = [blocks[index]]
+    for step in range(1, size):
+        sent = blocks[(index + step) % size]
+        done.append(lax.ppermute(sent, axis, [(i, (i + step) % size) for i in range(size)]))
+    blocks = jnp.stack(done)[(index - jnp.arange(size)) % size]
+    return laid_out(blocks, concat_dim)
 
 
 def rms_norm(values_f32, gain):
@@ -42,7 +65,7 @@
     returned = lax.all_to_all(looked, "rows", split_axis=0, concat_axis=0, tiled=True)
     embedded = returned.reshape(row_count * capacity, col_width)[slot_index]
     embedded = embedded.reshape(batch_dev, full_len, col_width)
-    sequence = lax.all_to_all(embedded, "cols", split_axis=1, concat_axis=2, tiled=True)
+    sequence = exchange_directly(embedded, "cols", 1, 2)
     residual = sequence.astype(jnp.float32)
     normed = rms_norm(residual, attn_gain).astype(jnp.bfloat16)
     projected = jnp.einsum("bqe,ef->bqf", normed, w_qkv, preferred_element_type=jnp.float32).astype(

time: 415 us -> 404 us (0.973)
  blocking collectives: 50.8 us -> 23.6 us
  waiting for transfers between devices: 135 us -> 153 us
  local copies, waits for them, and re-layouts: 90.2 us -> 83.6 us
    all_to_all x1 -> x0, blocking collectives: 27.2 us -> none  [local(): lax.all_to_all(embedded, 'cols', split_axis=1, concat_axis=2, tiled=True)]
    ppermute x0 -> x3, waiting for transfers between devices: none -> 14.5 us  [exchange_directly(): lax.ppermute(sent, axis, [(i, (i + step) % size) for i in range(size)])]
    reshape x1 -> x0, local copies, waits for them, and re-layouts: 8.68 us -> none  [local(): embedded = embedded.reshape(batch_dev, full_len, col_width)]
  transfers between devices with their start and end apart: 3 -> 6, of which waited for: 3 -> 4; matrix products, arithmetic and copies ran while one was open for 15% -> 15% of each run, Pallas kernels for 0% -> 0%
where the time goes in v1:
time: 404 us; the launch traced here: 403 us
  waiting for transfers between devices  153 us (38%)
  local copies, waits for them, and re-layouts  83.6 us (21%)
  matrix products  77.4 us (19%)
  other arithmetic  43.6 us (11%)
  blocking collectives  23.6 us (6%)
  between operations  13.7 us (3%)
  starting transfers between devices  8.5 us (2%)
    all_gather x1, waiting for transfers between devices, local(): key_piece = lax.all_gather(keys, 'cols', axis=1, tiled=True)  79.9 us
    all_to_all x1, waiting for transfers between devices, local(): lax.all_to_all(looked, 'rows', split_axis=0, concat_axis=0, tiled=True)  34.1 us
    gather x2, local copies, waits for them, and re-layouts, local(): looked = jnp.take(table, jnp.maximum(asked, 0), axis=0)  27.9 us
    dot_general x1, matrix products, local(): jnp.einsum('bqhd,bkhd->bhqk', queries, key_heads, preferred_element_type=...  27.7 us
    dot_general x1, matrix products, local(): jnp.einsum('bhqk,bkhd->bhqd', probs.astype(jnp.bfloat16), value_heads, pr...  27 us
    all_gather x1, waiting for transfers between devices, local(): value_piece = lax.all_gather(values, 'cols', axis=1, tiled=True)  24.5 us
    reduce_sum x1, other arithmetic, local(): running_sum = jnp.sum(probs, axis=-1)  22.4 us
    scatter x1, local copies, waits for them, and re-layouts, local(): requests = requests.at[slot_index].set(flat_ids - owner_block * block_row...  15.5 us
  transfers between devices with their start and end apart: 6, of which 4 were waited for; matrix products, arithmetic and copies ran while one was open for 15% of the time, Pallas kernels for 0%

profile of v1, /device:TPU:0, one launch (start us, length us, event | category | flops | bytes accessed | tf_op | source)
XLA Modules:
  0.0 403.5 jit_solution(5449553656300063628)
XLA Ops:
  6.5 15.2 %all_gather.9 = s32[2,2048]{1,0:T(2,128)S(1)} all-gather(s32[2,512]{1,0:T(2,128)} %param.9), channel_id=1, replica_groups=mesh['rows'=8,'cols'=4] {'cols'}, dimensions={1}, use_global_device_ids=true | all-gather | bytes 20480 | tf_op jit(solution)/shard_map/all_gather | solution.py:46
  21.8 2.3 reduce-window.6
  25.0 15.5 %scatter_custom_fusion = s32[10920]{0:T(1024)S(1)} fusion(s32[4096]{0:T(1024)S(1)} %bitcast.95, s32[4096]{0:T(1024)S(1)} %get-tuple-element.14, s32[]{:T(128)} %constant.85.clone.1), kind=kCustom, calls=%fused_computation.72 | custom fusion | bytes 43684 | tf_op jit(solution)/shard_map/scatter | solution.py:59
  40.6 8.4 %all_to_all.14 = s32[8,1,1365]{2,1,0:T(1,128)S(1)} all-to-all(s32[8,1,1365]{2,1,0:T(1,128)S(1)} %all_to_all.9), channel_id=1, replica_groups=mesh['rows'=8,'cols'=4] {'rows'}, dimensions={0} | all-to-all | bytes 87360 | tf_op jit(solution)/shard_map/all_to_all | solution.py:62
  49.2 23.7 %gather_fusion = bf16[10920,128]{1,0:T(8,128)(2,1)} fusion(bf16[16384,128]{1,0:T(8,128)(2,1)} %param.11, s32[11264]{0:T(1024)S(1)} %pad_clamp_fusion), kind=kCustom, calls=%fused_computation | custom fusion | bytes 5634720 | tf_op jit(solution)/shard_map/jit(_take)/gather | solution.py:63
  72.9 4.2 %reshape.311 = bf16[8,1365,128]{2,1,0:T(8,128)(2,1)} reshape(bf16[10920,128]{1,0:T(8,128)(2,1)} %gather_fusion) | data formatting | bytes 5591040 | tf_op jit(solution)/shard_map/jit(_take)/gather | solution.py:63
  77.1 10.2 %select_select_fusion = bf16[8,1365,128]{2,1,0:T(8,128)(2,1)} fusion(bf16[8,1365,128]{2,1,0:T(8,128)(2,1)} %reshape.311, pred[8,1365]{1,0:T(8,128)(4,1)S(1)} %get-tuple-element.13, pred[8,1365]{1,0:T(8,128)(4,1)S(1)} %get-tuple-element.12), kind=kLoop, calls=%fused_computation.22 | loop fusion | flops 2795520 | bytes 5612880 | tf_op jit(solution)/shard_map/jit(_where)/select_n | solution.py:64
  87.3 4.4 %all-to-all-start.1 = ((bf16[8,1365,128]{2,1,0:T(8,128)(2,1)}), bf16[8,1365,128]{2,1,0:T(8,128)(2,1)}, u32[]{:S(2)}, u32[]{:S(2)}) async-start(bf16[8,1365,128]{2,1,0:T(8,128)(2,1)} %select_select_fusion), calls=%async_computation.1 | async-start | bytes 5603328 | tf_op jit(solution)/shard_map/all_to_all | solution.py:65
  91.8 34.1 %all-to-all-done.1 = bf16[8,1365,128]{2,1,0:T(8,128)(2,1)} async-done(((bf16[8,1365,128]{2,1,0:T(8,128)(2,1)}), bf16[8,1365,128]{2,1,0:T(8,128)(2,1)}, u32[]{:S(2)}, u32[]{:S(2)}) %all-to-all-start.1) | async-done | bytes 2795552 | tf_op jit(solution)/shard_map/all_to_all | solution.py:65
  125.9 4.2 %reshape.305 = bf16[10920,128]{1,0:T(8,128)(2,1)} reshape(bf16[8,1365,128]{2,1,0:T(8,128)(2,1)} %all-to-all-done.1) | data formatting | bytes 5591040 | tf_op jit(solution)/shard_map/reshape | solution.py:66
  130.1 13.2 %gather_fusion.1 = bf16[4096,128]{1,0:T(8,128)(2,1)S(1)} fusion(bf16[10920,128]{1,0:T(8,128)(2,1)} %reshape.305, s32[4096]{0:T(1024)S(1)} %broadcast_clamp_fusion), kind=kCustom, calls=%fused_computation.1 | custom fusion | bytes 2113536 | tf_op jit(solution)/shard_map/gather | solution.py:66
  144.0 3.4 collective-permute-start.2
  147.4 14.5 %collective-permute-done.1 = bf16[2,512,128]{2,1,0:T(8,128)(2,1)S(1)} collective-permute-done((bf16[2,512,128]{2,1,0:T(8,128)(2,1)S(1)}, bf16[2,512,128]{2,1,0:T(8,128)(2,1)S(1)}, u32[]{:S(2)}, u32[]{:S(2)}) %collective-permute-start.1) | collective-permute-done | bytes 262176 | tf_op jit(solution)/shard_map/ppermute | solution.py:29
  163.1 2.0 gather_fusion.2
  165.1 1.5 convert_bitcast_fusion
  166.8 2.9 copy.41
  169.8 1.8 fusion.19
  171.6 3.2 convolution_convert_fusion
  174.9 1.7 fusion.47
  177.4 2.6 broadcast_and_fusion
  180.0 1.3 copy.43
  181.4 79.9 %all-gather.3.cloned.1.call-done = bf16[2,2048,512]{2,1,0:T(8,128)(2,1)} async-done(((bf16[2,512,512]{2,1,0:T(8,128)(2,1)}), bf16[2,2048,512]{2,1,0:T(8,128)(2,1)}) %all-gather.3.cloned.1.call-update) | async-done | bytes 4194320 | tf_op jit(solution)/shard_map/all_gather | solution.py:80
  261.3 6.3 %copy.44 = bf16[2,2048,512]{1,2,0:T(8,128)(2,1)} copy(bf16[2,2048,512]{2,1,0:T(8,128)(2,1)} %all-gather.3.cloned.1.call-done) | data formatting | bytes 8388608 | tf_op jit(solution)/shard_map/all_gather | solution.py:80
  267.6 27.7 %fusion = (f32[2,8,512]{2,1,0:T(8,128)S(1)}, f32[2,8,512,2048]{3,2,1,0:T(8,128)}) fusion(pred[2,512,2048]{2,1,0:T(8,128)(4,1)} %broadcast_and_fusion, bf16[2,512,8,64]{1,3,2,0:T(8,128)(2,1)} %bitcast.85, bf16[2,2048,8,64]{1,3,2,0:T(8,128)(2,1)} %bitcast.84), kind=kOutput, calls=%fused_computation.6 | convolution fusion | flops 2197807104 | bytes 74481664 | tf_op jit(solution)/shard_map/bqhd,bkhd->bhqk/dot_general | solution.py:86
  295.3 22.4 %fusion.1 = f32[2,8,512]{2,1,0:T(8,128)S(1)} fusion(f32[2,8,512,2048]{3,2,1,0:T(8,128)} %get-tuple-element.17, f32[2,8,512]{2,1,0:T(8,128)S(1)} %broadcast_maximum_fusion, pred[2,512,2048]{2,1,0:T(8,128)(4,1)S(1)} %copy-done.1), kind=kLoop, calls=%fused_computation.7 | loop fusion | flops 83877888 | bytes 69271552 | tf_op jit(solution)/shard_map/reduce_sum | solution.py:96
  317.6 24.5 %all-gather.5.cloned.1.call-done = bf16[2,2048,512]{2,1,0:T(8,128)(2,1)} async-done(((bf16[2,512,512]{2,1,0:T(8,128)(2,1)}), bf16[2,2048,512]{2,1,0:T(8,128)(2,1)}) %all-gather.5.cloned.1.call-update) | async-done | bytes 4194320 | tf_op jit(solution)/shard_map/all_gather | solution.py:81
  342.1 6.3 %copy.45 = bf16[2,2048,512]{1,2,0:T(8,128)(2,1)} copy(bf16[2,2048,512]{2,1,0:T(8,128)(2,1)} %all-gather.5.cloned.1.call-done) | data formatting | bytes 8388608 | tf_op jit(solution)/shard_map/all_gather | solution.py:81
  348.4 27.0 %fusion.17 = bf16[2,512,8,64]{1,3,2,0:T(8,128)(2,1)S(1)} fusion(bf16[2,2048,8,64]{1,3,2,0:T(8,128)(2,1)} %bitcast.87, f32[2,8,512,2048]{3,2,1,0:T(8,128)} %get-tuple-element.17, f32[2,8,512]{2,1,0:T(8,128)S(1)} %broadcast_maximum_fusion, pred[2,512,2048]{2,1,0:T(8,128)(4,1)} %broadcast_and_fusion, f32[2,512,8]{1,2,0:T(8,128)S(1)} %bitcast.99), kind=kOutput, calls=%fused_computation.32 | convolution fusion | flops 2232418304 | bytes 74514432 | tf_op jit(solution)/shard_map/bhqk,bkhd->bhqd/dot_general | solution.py:97
  375.4 2.7 fusion.12
  378.4 8.3 %fusion.7 = f32[2,512,4096]{2,1,0:T(8,128)} fusion(bf16[512,4096]{1,0:T(8,128)(2,1)S(1)} %copy-done.4, bf16[2,512,512]{1,2,0:T(8,128)(2,1)S(1)} %get-tuple-element.19, f32[512]{0:T(512)S(1)} %copy-done.5, f32[2,512]{1,0:T(2,128)S(1)} %add_rsqrt_fusion), kind=kOutput, calls=%fused_computation.13 | convolution fusion | flops 4297064448 | bytes 22026240 | tf_op jit(solution)/shard_map/bqe,ef->bqf/dot_general | solution.py:113
  386.7 8.6 %fusion.15 = bf16[2,512,512]{1,2,0:T(8,128)(2,1)S(1)} fusion(bf16[2,512,512]{1,2,0:T(8,128)(2,1)S(1)} %get-tuple-element.19, bf16[2048,512]{1,0:T(8,128)(2,1)S(1)} %copy-done, f32[2,512,4096]{2,1,0:T(8,128)} %fusion.7), kind=kOutput, calls=%fused_computation.29 | convolution fusion | flops 2161639424 | bytes 20971520 | tf_op jit(solution)/shard_map/bqf,fe->bqe/dot_general | solution.py:116
  395.3 1.3 copy.50
  (48 shorter events, 4.4 us)
Async XLA Ops:
  6.5 380.2 %copy-start = (bf16[2048,512]{1,0:T(8,128)(2,1)S(1)}, bf16[2048,512]{1,0:T(8,128)(2,1)}, u32[]{:S(2)}) copy-start(bf16[2048,512]{1,0:T(8,128)(2,1)} %param.17) | copy-start | bytes 6291460
  87.3 38.6 %all-to-all-start.1 = ((bf16[8,1365,128]{2,1,0:T(8,128)(2,1)}), bf16[8,1365,128]{2,1,0:T(8,128)(2,1)}, u32[]{:S(2)}, u32[]{:S(2)}) async-start(bf16[8,1365,128]{2,1,0:T(8,128)(2,1)} %select_select_fusion), calls=%async_computation.1 | async-start | bytes 5603328 | tf_op jit(solution)/shard_map/all_to_all | solution.py:65
  91.7 169.6 %all-gather.3.cloned.1.call-start = ((), (), s32[]{:S(2)}) async-start(), calls=%async_computation.2 | async-start | bytes 5242880 | tf_op jit(solution)/shard_map/all_gather | solution.py:80
  143.4 18.6 %collective-permute-start.1 = (bf16[2,512,128]{2,1,0:T(8,128)(2,1)S(1)}, bf16[2,512,128]{2,1,0:T(8,128)(2,1)S(1)}, u32[]{:S(2)}, u32[]{:S(2)}) collective-permute-start(bf16[2,512,128]{2,1,0:T(8,128)(2,1)S(1)} %get-tuple-element.10), channel_id=1, source_target_pairs={{0,2},{1,3},{2,0},{3,1},{4,6},{5,7},{6,4},{7,5},{8,10},{9,11},{10,... | collective-permute-start | bytes 786440 | tf_op jit(solution)/shard_map/ppermute | solution.py:29
  144.0 17.9 %collective-permute-start.2 = (bf16[2,512,128]{2,1,0:T(8,128)(2,1)S(1)}, bf16[2,512,128]{2,1,0:T(8,128)(2,1)S(1)}, u32[]{:S(2)}, u32[]{:S(2)}) collective-permute-start(bf16[2,512,128]{2,1,0:T(8,128)(2,1)S(1)} %get-tuple-element.9), channel_id=1, source_target_pairs={{0,3},{1,0},{2,1},{3,2},{4,7},{5,4},{6,5},{7,6},{8,11},{9,8},{10,9... | collective-permute-start | bytes 786440 | tf_op jit(solution)/shard_map/ppermute | solution.py:29
  147.4 14.6 %collective-permute-start = (bf16[2,512,128]{2,1,0:T(8,128)(2,1)S(1)}, bf16[2,512,128]{2,1,0:T(8,128)(2,1)S(1)}, u32[]{:S(2)}, u32[]{:S(2)}) collective-permute-start(bf16[2,512,128]{2,1,0:T(8,128)(2,1)S(1)} %get-tuple-element.11), channel_id=1, source_target_pairs={{0,1},{1,2},{2,3},{3,0},{4,5},{5,6},{6,7},{7,4},{8,9},{9,10},{10,1... | collective-permute-start | bytes 786440 | tf_op jit(solution)/shard_map/ppermute | solution.py:29
  165.1 4.7 %copy-start.2 = (f32[512]{0:T(512)S(1)}, f32[512]{0:T(512)}, u32[]{:S(2)}) copy-start(f32[512]{0:T(512)} %param.12) | copy-start | bytes 6148
  174.9 1.8 copy-start.3
  176.6 165.6 %all-gather.5.cloned.1.call-start = ((), (), s32[]{:S(2)}) async-start(), calls=%async_computation.3 | async-start | bytes 5242880 | tf_op jit(solution)/shard_map/all_gather | solution.py:81
  267.6 27.7 %copy-start.1 = (pred[2,512,2048]{2,1,0:T(8,128)(4,1)S(1)}, pred[2,512,2048]{2,1,0:T(8,128)(4,1)}, u32[]{:S(2)}) copy-start(pred[2,512,2048]{2,1,0:T(8,128)(4,1)} %broadcast_and_fusion) | copy-start | bytes 6291460
  375.4 3.0 copy-start.4
  375.4 3.0 copy-start.5
Sparse Core Ops, SparseCore 0:
  176.7 84.5 all-gather.2
  262.9 79.2 all-gather.4
